TPU v7x, 32 devices: a whole 2x2x4 slice. The times are simulated.
32 devices in a mesh: patch: 16 (over z, x, core), tp: 2 (over y).
Axes of the slice: x: 2, y: 2, z: 4, core: 2. Of those that a mesh axis runs over, the one named last changes fastest.
Arguments:
- resid_corrupt: bfloat16 [512, 4096], P(None, 'tp'), may hold values from -6 to 6
- resid_clean: bfloat16 [2, 512, 4096], P(None, 'patch', 'tp'), may hold values from -6 to 6
- patch_level: int32 [16], P('patch'), may hold values from 0 to 1
- patch_mask: int32 [16, 128], P('patch'), may hold values 0 or 1
- norm_gain: bfloat16 [4096], P('tp'), may hold values from 0.099609375 to 1.8984375
- final_gain: bfloat16 [4096], P('tp'), may hold values from 0.099609375 to 1.8984375
- w_query: bfloat16 [4096, 4096], P('patch', 'tp'), may hold values from -1 to 1
- w_key: bfloat16 [4096, 1024], P('patch', 'tp'), may hold values from -1 to 1
- w_value: bfloat16 [4096, 1024], P('patch', 'tp'), may hold values from -0.09375 to 0.09375
- w_out: bfloat16 [4096, 4096], P('tp', 'patch'), may hold values from -0.09375 to 0.09375
- unembed: bfloat16 [128256, 4096], P(('patch', 'tp')), may hold values from -0.09375 to 0.09375
- scored_ids: int32 [256], replicated, may hold values from 0 to 128255
- base_logits: float32 [512, 256], P('tp'), may hold values from -6 to 6
Outputs:
- logit_shift: float32 [16, 512, 256], P('patch', 'tp')
All inputs are finite; a program needn't handle non-finite values. No bound on the sum of `patch_mask` on one device may be relied on, other than what follows from the above.
Results may differ from a plain program's by a relative error of at most 0.01.
The roundings to bfloat16 on the way count: a program that leaves them out, or rounds other values in their place, can miss the bound.
Values may be sent and summed in bfloat16 or wider, within the bound.
No kernel may reach another device: no remote copies, remote signals or barrier semaphores. Data moves between devices by JAX's collectives and lax.ppermute only.
A program may use at most 192 MiB of HBM per device.

v0:
```python
import jax
import jax.numpy as jnp
from jax import lax
from jax.sharding import PartitionSpec as P

D = 4096
HD = 128
SEQ = 128
PROMPTS = 4
EPSILON = 1e-05
THETA = 500000.0


def rope_tables(length, head_dim):
    half = head_dim // 2
    freqs = THETA ** (-(jnp.arange(half, dtype=jnp.float32) * 2.0 / head_dim))
    angles = jnp.arange(length, dtype=jnp.float32)[:, None] * freqs[None, :]
    return (jnp.cos(angles)[:, None, :], jnp.sin(angles)[:, None, :])


def rotate(values, cosine, sine):
    half = values.shape[-1] // 2
    lower = values[..., :half]
    upper = values[..., half:]
    return jnp.concatenate([lower * cosine - upper * sine, upper * cosine + lower * sine], axis=-1)


def rms_scale(rows, gain):
    return rows * lax.rsqrt(jnp.mean(rows * rows, axis=-1, keepdims=True) + EPSILON) * gain


def attend(query_f, key_f, value_f):
    heads = query_f.shape[1] // HD
    kv_heads = key_f.shape[1] // HD
    group = heads // kv_heads
    prompts = query_f.shape[0] // SEQ
    cosine, sine = rope_tables(SEQ, HD)
    queries = rotate(query_f.reshape(prompts, SEQ, heads, HD), cosine, sine).astype(jnp.bfloat16)
    queries = queries.reshape(prompts, SEQ, kv_heads, group, HD)
    key_rows = rotate(key_f.reshape(prompts, SEQ, kv_heads, HD), cosine, sine).astype(jnp.bfloat16)
    value_rows = value_f.astype(jnp.bfloat16).reshape(prompts, SEQ, kv_heads, HD)
    scores = jnp.einsum(
        "pqkgd,pskd->pkgqs", queries, key_rows, preferred_element_type=jnp.float32
    ) * HD ** (-0.5)
    causal = lax.iota(jnp.int32, SEQ)[:, None] >= lax.iota(jnp.int32, SEQ)[None, :]
    scores = jnp.where(causal, scores, -1e30)
    probs = jax.nn.softmax(scores, axis=-1).astype(jnp.bfloat16)
    attended = jnp.einsum(
        "pkgqs,pskd->pqkgd", probs, value_rows, preferred_element_type=jnp.float32
    )
    return attended.astype(jnp.bfloat16).reshape(prompts * SEQ, heads * HD)


def on_device(
    resid_corrupt,
    resid_clean,
    patch_level,
    patch_mask,
    norm_gain,
    final_gain,
    w_query,
    w_key,
    w_value,
    w_out,
    unembed,
    scored_ids,
    base_logits,
):
    level = patch_level[0]
    row_mask = jnp.tile(patch_mask[0], PROMPTS) == 1
    clean_all = lax.all_gather(resid_clean, "patch", axis=1, tiled=True)
    early = (row_mask & (level == 0))[:, None]
    layer_in = jnp.where(early, clean_all[0], resid_corrupt)
    full_rows, full_gain = (
        lax.all_gather(layer_in, "tp", axis=1, tiled=True),
        lax.all_gather(norm_gain, "tp", axis=0, tiled=True),
    )
    normed = rms_scale(full_rows.astype(jnp.float32), full_gain.astype(jnp.float32)).astype(
        jnp.bfloat16
    )
    query_f = jnp.dot(
        normed,
        lax.all_gather(w_query, "patch", axis=0, tiled=True),
        preferred_element_type=jnp.float32,
    )
    key_f = jnp.dot(
        normed,
        lax.all_gather(w_key, "patch", axis=0, tiled=True),
        preferred_element_type=jnp.float32,
    )
    value_f = jnp.dot(
        normed,
        lax.all_gather(w_value, "patch", axis=0, tiled=True),
        preferred_element_type=jnp.float32,
    )
    attended = attend(query_f, key_f, value_f)
    partial_out = jnp.dot(
        attended,
        lax.all_gather(w_out, "patch", axis=1, tiled=True),
        preferred_element_type=jnp.float32,
    )
    head_block = lax.psum_scatter(
        partial_out.astype(jnp.bfloat16), "tp", scatter_dimension=1, tiled=True
    ).astype(jnp.float32)
    middle = layer_in.astype(jnp.float32) + head_block
    late = (row_mask & (level == 1))[:, None]
    residual = jnp.where(late, clean_all[1].astype(jnp.float32), middle)
    squares = lax.psum(jnp.sum(residual * residual, axis=1), "tp")
    scaling = lax.rsqrt(squares / D + EPSILON)[:, None]
    final_block = (residual * scaling * final_gain.astype(jnp.float32)).astype(jnp.bfloat16)
    rows_dev = unembed.shape[0]
    first_row = lax.axis_index(("patch", "tp")) * rows_dev
    owned_rows = (scored_ids[:, None] == first_row + lax.iota(jnp.int32, rows_dev)[None, :]).astype(
        jnp.bfloat16
    )
    picked = jnp.dot(owned_rows, unembed, preferred_element_type=jnp.float32)
    tp_count = lax.axis_size("tp")
    patch_count = lax.axis_size("patch")
    fine = picked.shape[1] // (tp_count * patch_count)
    reordered = (
        picked.reshape(picked.shape[0], tp_count, patch_count, fine)
        .transpose(0, 2, 1, 3)
        .reshape(picked.shape)
    )
    small_block = lax.psum_scatter(
        reordered, ("patch", "tp"), scatter_dimension=1, tiled=True
    ).astype(jnp.bfloat16)
    score_block = lax.all_gather(small_block, "patch", axis=1, tiled=True)
    partial_logits = jnp.einsum(
        "td,sd->ts", final_block, score_block, preferred_element_type=jnp.float32
    )
    token_logits = lax.psum_scatter(
        partial_logits.astype(jnp.bfloat16), "tp", scatter_dimension=0, tiled=True
    ).astype(jnp.float32)
    return (token_logits - base_logits)[None]


def solution(mesh):
    placed = (
        P(None, "tp"),
        P(None, "patch", "tp"),
        P("patch"),
        P("patch", None),
        P("tp"),
        P("tp"),
        P("patch", "tp"),
        P("patch", "tp"),
        P("patch", "tp"),
        P("tp", "patch"),
        P(("patch", "tp"), None),
        P(),
        P("tp", None),
    )
    return jax.shard_map(
        on_device, mesh=mesh, in_specs=placed, out_specs=P("patch", "tp", None), check_vma=False
    )
```

profile of v0, /device:TPU:0, one launch (start us, length us, event | category | flops | bytes accessed | tf_op | source)
XLA Modules:
  0.0 590.9 jit_solution(3433923609739333319)
XLA Ops:
  7.4 0.0 all-gather.8.cloned.1.call-start
  7.4 0.7 all-gather.8.cloned.1.call-update
  8.1 0.0 all-gather.10.cloned.1.call-start
  8.8 0.7 and_bitcast_fusion.1
  9.5 54.0 %all-gather.8.cloned.1.call-done = bf16[2,512,2048]{2,1,0:T(8,128)(2,1)} async-done(((bf16[2,32,2048]{2,1,0:T(8,128)(2,1)}), bf16[2,512,2048]{2,1,0:T(8,128)(2,1)}) %all-gather.8.cloned.1.call-update) | async-done | bytes 4194320 | tf_op jit(solution)/shard_map/all_gather | solution.py:71
  63.5 3.9 fusion.11
  67.4 0.0 all-gather.10.cloned.1.call-update
  67.4 0.0 all-gather.14.cloned.1.call-start
  67.5 0.7 all-gather.14.cloned.1.call-update
  68.2 0.0 all-gather.12.cloned.1.call-start
  68.2 0.5 all-gather.12.cloned.1.call-update
  68.7 0.0 all-gather.16.cloned.1.call-start
  68.8 0.5 all-gather.16.cloned.1.call-update
  69.3 0.0 all-gather.18.cloned.1.call-start
  69.4 0.5 all-gather.18.cloned.1.call-update
  69.9 0.0 reduce-scatter.6.cloned.1.call-start
  70.0 0.0 copy-done.4
  70.0 17.1 %fusion.7 = f32[32,8,32,128]{3,1,2,0:T(8,128)S(1)} fusion(bf16[4008,4096]{1,0:T(8,128)(2,1)} %param.23, s32[4008]{0:T(1024)S(1)} %iota_add_fusion, s32[256]{0:T(256)S(1)} %copy-done.4), kind=kOutput, calls=%fused_computation.18 | convolution fusion | flops 8406411264 | bytes 37044896 | tf_op jit(solution)/shard_map/dot_general | solution.py:116
  87.1 2.7 copy.44
  89.8 5.3 copy.35
  95.1 0.0 reduce-scatter.6.cloned.1.call-update
  95.1 0.0 reduce-scatter.4.cloned.1.call-start
  95.2 0.6 copy-done.2
  95.8 4.7 all_gather.26
  100.5 0.3 fusion.30
  100.8 23.2 %all-gather.10.cloned.1.call-done = bf16[512,4096]{1,0:T(8,128)(2,1)} async-done(((bf16[512,2048]{1,0:T(8,128)(2,1)}), bf16[512,4096]{1,0:T(8,128)(2,1)}) %all-gather.10.cloned.1.call-update) | async-done | bytes 4194320 | tf_op jit(solution)/shard_map/all_gather | solution.py:75
  123.9 3.1 fusion.1
  127.0 50.4 %all-gather.14.cloned.1.call-done = bf16[4096,512]{1,0:T(8,128)(2,1)} async-done(((bf16[256,512]{1,0:T(8,128)(2,1)}), bf16[4096,512]{1,0:T(8,128)(2,1)}) %all-gather.14.cloned.1.call-update) | async-done | bytes 4194320 | tf_op jit(solution)/shard_map/all_gather | solution.py:88
  177.5 5.8 fusion.35
  183.3 0.4 reshape.117
  183.7 0.6 fusion.38
  184.3 45.9 %all-gather.12.cloned.1.call-done = bf16[4096,512]{1,0:T(8,128)(2,1)} async-done(((bf16[256,512]{1,0:T(8,128)(2,1)}), bf16[4096,512]{1,0:T(8,128)(2,1)}) %all-gather.12.cloned.1.call-update) | async-done | bytes 4194320 | tf_op jit(solution)/shard_map/all_gather | solution.py:93
  230.2 6.6 %convolution_convert_fusion.1 = bf16[512,512]{1,0:T(8,128)(2,1)} fusion(bf16[4096,512]{1,0:T(8,128)(2,1)} %all-gather.12.cloned.1.call-done, bf16[512,4096]{1,0:T(8,128)(2,1)} %all-gather.10.cloned.1.call-done, f32[4096]{0:T(1024)S(1)} %convert_element_type.59, f32[512]{0:T(512)S(1)} %add_rsqrt_fusion.1), kind=kOutput, calls=%fused_computation.38 | convolution fusion | flops 2156134400 | bytes 8931328 | tf_op jit(solution)/shard_map/dot_general | solution.py:91
  236.8 0.3 subtract_convert_fusion.1
  237.1 1.2 reshape.116
  238.3 120.7 %all-gather.16.cloned.1.call-done = bf16[4096,2048]{1,0:T(8,128)(2,1)} async-done(((bf16[256,2048]{1,0:T(8,128)(2,1)}), bf16[4096,2048]{1,0:T(8,128)(2,1)}) %all-gather.16.cloned.1.call-update) | async-done | bytes 16777232 | tf_op jit(solution)/shard_map/all_gather | solution.py:83
  359.0 13.3 %convolution_bitcast_fusion = f32[64,8,16,128]{3,1,2,0:T(8,128)S(1)} fusion(bf16[4096,2048]{1,0:T(8,128)(2,1)} %all-gather.16.cloned.1.call-done, bf16[512,4096]{1,0:T(8,128)(2,1)} %all-gather.10.cloned.1.call-done, f32[4096]{0:T(1024)S(1)} %convert_element_type.59, f32[512]{0:T(512)S(1)} %add_rsqrt_fusion.1), kind=kOutput, calls=%fused_computation.19 | convolution fusion | flops 8598323200 | bytes 25184256 | tf_op jit(solution)/shard_map/dot_general | solution.py:81
  372.3 0.9 copy.43
  373.2 1.4 subtract_convert_fusion
  374.6 0.5 copy.31
  375.2 0.5 copy.30
  375.7 1.6 fusion.12
  377.3 1.1 fusion.39
  378.4 2.1 convert_bitcast_fusion
  380.5 3.4 copy.34
  384.0 2.8 reshape.119
  386.8 103.3 %all-gather.18.cloned.1.call-done = bf16[2048,4096]{1,0:T(8,128)(2,1)} async-done(((bf16[2048,256]{1,0:T(8,128)(2,1)}), bf16[2048,4096]{1,0:T(8,128)(2,1)}) %all-gather.18.cloned.1.call-update) | async-done | bytes 16777232 | tf_op jit(solution)/shard_map/all_gather | solution.py:99
  490.1 14.3 %convolution_convert_fusion = bf16[512,4096]{1,0:T(8,128)(2,1)} fusion(bf16[512,2048]{1,0:T(8,128)(2,1)} %reshape.119, bf16[2048,4096]{1,0:T(8,128)(2,1)} %all-gather.18.cloned.1.call-done), kind=kOutput, calls=%fused_computation.6 | convolution fusion | flops 8592031744 | bytes 23068672 | tf_op jit(solution)/shard_map/dot_general | solution.py:97
  504.5 0.0 reduce-scatter.4.cloned.1.call-update
  504.5 0.0 all-gather.20.cloned.1.call-start
  504.5 0.0 reduce-scatter.6.cloned.1.call-done
  504.6 1.7 convert_element_type.69
  506.2 0.0 all-gather.20.cloned.1.call-update
  506.3 0.0 reduce-scatter.8.cloned.1.call-start
  506.3 0.0 copy-done.3
  506.4 50.7 %reduce-scatter.4.cloned.1.call-done = bf16[512,2048]{1,0:T(8,128)(2,1)} async-done(((bf16[512,4096]{1,0:T(8,128)(2,1)}), bf16[512,2048]{1,0:T(8,128)(2,1)}) %reduce-scatter.4.cloned.1.call-update) | async-done | bytes 2097168 | tf_op jit(solution)/shard_map/reduce_scatter | solution.py:102
  557.1 0.0 copy-done
  557.1 3.3 multiply_reduce_fusion
  560.4 4.9 psum.7
  565.3 0.0 all-gather.20.cloned.1.call-done
  565.3 4.5 fusion.25
  569.8 0.0 reduce-scatter.8.cloned.1.call-update
  569.8 11.8 %reduce-scatter.8.cloned.1.call-done = bf16[256,256]{1,0:T(8,128)(2,1)} async-done(((bf16[512,256]{1,0:T(8,128)(2,1)}), bf16[256,256]{1,0:T(8,128)(2,1)}) %reduce-scatter.8.cloned.1.call-update) | async-done | bytes 131088 | tf_op jit(solution)/shard_map/reduce_scatter | solution.py:132
  581.7 1.6 subtract_bitcast_fusion
  (15 shorter events, 0.1 us)
Async XLA Ops:
  7.4 56.1 %all-gather.8.cloned.1.call-start = ((), (), s32[]{:S(2)}) async-start(), calls=%async_computation.3 | async-start | bytes 4456448 | tf_op jit(solution)/shard_map/all_gather | solution.py:71
  8.1 115.9 %all-gather.10.cloned.1.call-start = ((), (), s32[]{:S(2)}) async-start(), calls=%async_computation.4 | async-start | bytes 6291456 | tf_op jit(solution)/shard_map/all_gather | solution.py:75
  9.5 60.5 %copy-start.4 = (s32[256]{0:T(256)S(1)}, s32[256]{0:T(256)}, u32[]{:S(2)}) copy-start(s32[256]{0:T(256)} %param.24) | copy-start | bytes 3076
  67.4 110.0 %all-gather.14.cloned.1.call-start = ((), (), s32[]{:S(2)}) async-start(), calls=%async_computation.6 | async-start | bytes 4456448 | tf_op jit(solution)/shard_map/all_gather | solution.py:88
  68.2 162.0 %all-gather.12.cloned.1.call-start = ((), (), s32[]{:S(2)}) async-start(), calls=%async_computation.5 | async-start | bytes 4456448 | tf_op jit(solution)/shard_map/all_gather | solution.py:93
  68.7 290.2 %all-gather.16.cloned.1.call-start = ((), (), s32[]{:S(2)}) async-start(), calls=%async_computation.7 | async-start | bytes 17825792 | tf_op jit(solution)/shard_map/all_gather | solution.py:83
  69.3 420.8 %all-gather.18.cloned.1.call-start = ((), (), s32[]{:S(2)}) async-start(), calls=%async_computation.8 | async-start | bytes 17825792 | tf_op jit(solution)/shard_map/all_gather | solution.py:99
  69.9 434.7 %reduce-scatter.6.cloned.1.call-start = ((), (), s32[]{:S(2)}) async-start(), calls=%async_computation.10 | async-start | bytes 4325376 | tf_op jit(solution)/shard_map/reduce_scatter | solution.py:125
  95.1 0.7 copy-start.2
  95.1 462.0 %reduce-scatter.4.cloned.1.call-start = ((), (), s32[]{:S(2)}) async-start(), calls=%async_computation.9 | async-start | bytes 6291456 | tf_op jit(solution)/shard_map/reduce_scatter | solution.py:102
  504.5 1.9 copy-start.3
  504.5 52.6 %copy-start = (bf16[512,2048]{1,0:T(8,128)(2,1)S(1)}, bf16[512,2048]{1,0:T(8,128)(2,1)}, u32[]{:S(2)}) copy-start(bf16[512,2048]{1,0:T(8,128)(2,1)} %fusion.11) | copy-start | bytes 6291460
  504.5 60.8 %all-gather.20.cloned.1.call-start = ((), (), s32[]{:S(2)}) async-start(), calls=%async_computation.11 | async-start | bytes 1114112 | tf_op jit(solution)/shard_map/all_gather | solution.py:128
  506.3 75.4 %reduce-scatter.8.cloned.1.call-start = ((), (), s32[]{:S(2)}) async-start(), calls=%async_computation.12 | async-start | bytes 393216 | tf_op jit(solution)/shard_map/reduce_scatter | solution.py:132
  565.3 16.4 %copy-start.1 = (f32[256,256]{1,0:T(8,128)S(1)}, f32[256,256]{1,0:T(8,128)}, u32[]{:S(2)}) copy-start(f32[256,256]{1,0:T(8,128)} %param.25) | copy-start | bytes 786436
Sparse Core Ops, SparseCore 0:
  10.3 53.1 all-gather.7
  67.5 56.3 all-gather.9
  126.1 51.2 all-gather.13
  179.5 50.6 all-gather.11
  232.2 126.7 all-gather.15
  361.0 129.1 all-gather.17
  507.5 36.0 all-gather.19
Sparse Core Ops, SparseCore 1:
  95.2 264.9 reduce-scatter.5
  504.6 52.5 reduce-scatter.3
  569.9 11.7 reduce-scatter.7
where the time goes:
time: 591 us
  waiting for transfers between devices  463 us (78%)
  matrix products  65.4 us (11%)
  local copies, waits for them, and re-layouts  19 us (3%)
  other arithmetic  17.4 us (3%)
  between operations  15.9 us (3%)
  blocking collectives  9.67 us (2%)
    all_gather x1, waiting for transfers between devices, on_device(): lax.all_gather(w_query, 'patch', axis=0, tiled=True)  121 us
    all_gather x1, waiting for transfers between devices, on_device(): lax.all_gather(w_out, 'patch', axis=1, tiled=True)  103 us
    all_gather x1, waiting for transfers between devices, on_device(): clean_all = lax.all_gather(resid_clean, 'patch', axis=1, tiled=True)  54 us
    reduce_scatter x1, waiting for transfers between devices, on_device(): lax.psum_scatter(partial_out.astype(jnp.bfloat16), 'tp', scatter_dimensio...  50.7 us
    all_gather x1, waiting for transfers between devices, on_device(): lax.all_gather(w_key, 'patch', axis=0, tiled=True)  50.4 us
    all_gather x1, waiting for transfers between devices, on_device(): lax.all_gather(w_value, 'patch', axis=0, tiled=True)  45.9 us
    all_gather x1, waiting for transfers between devices, on_device(): lax.all_gather(layer_in, 'tp', axis=1, tiled=True)  23.2 us
    dot_general x1, matrix products, on_device(): picked = jnp.dot(owned_rows, unembed, preferred_element_type=jnp.float32)  17.1 us
  transfers between devices with their start and end apart: 10, of which 8 were waited for; matrix products, arithmetic and copies ran while one was open for 15% of the time, Pallas kernels for 0%

commit v1 on v0

--- a/solution.py
+++ b/solution.py
@@ -68,7 +68,15 @@
 ):
     level = patch_level[0]
     row_mask = jnp.tile(patch_mask[0], PROMPTS) == 1
-    clean_all = lax.all_gather(resid_clean, "patch", axis=1, tiled=True)
+    n_dev_all = lax.axis_size("patch")
+    sides = [(no, (no + 1) % n_dev_all) for no in range(n_dev_all)]
+    met_up = [None] * n_dev_all
+    met_up[n_dev_all - 1] = resid_clean
+    for src_i in range(n_dev_all - 2, -1, -1):
+        met_up[src_i] = lax.ppermute(met_up[src_i + 1], axis_name="patch", perm=sides)
+    left_arr = jnp.concatenate(met_up, axis=1)
+    side_arr = (lax.axis_index("patch") + 1) * resid_clean.shape[1]
+    clean_all = jnp.roll(left_arr, side_arr, 1)
     early = (row_mask & (level == 0))[:, None]
     layer_in = jnp.where(early, clean_all[0], resid_corrupt)
     full_rows, full_gain = (

time: 591 us -> 673 us (1.14)
  waiting for transfers between devices: 463 us -> 536 us
  local copies, waits for them, and re-layouts: 19 us -> 28.6 us
    ppermute x0 -> x15, waiting for transfers between devices: none -> 127 us  [on_device(): lax.ppermute(met_up[src_i + 1], axis_name='patch', perm=sides)]
    all_gather x1 -> x0, waiting for transfers between devices: 54 us -> none  [on_device(): clean_all = lax.all_gather(resid_clean, 'patch', axis=1, tiled=True)]
    unnamed x12 -> x53, local copies, waits for them, and re-layouts: 4.22 us -> 13.9 us
  transfers between devices with their start and end apart: 10 -> 24, of which waited for: 8 -> 22; matrix products, arithmetic and copies ran while one was open for 15% -> 14% of each run, Pallas kernels for 0% -> 0%
where the time goes in v1:
time: 673 us; the launch traced here: 672 us
  waiting for transfers between devices  536 us (80%)
  matrix products  65.5 us (10%)
  local copies, waits for them, and re-layouts  28.6 us (4%)
  between operations  16.2 us (2%)
  other arithmetic  15.2 us (2%)
  blocking collectives  9.68 us (1%)
    ppermute x15, waiting for transfers between devices, on_device(): lax.ppermute(met_up[src_i + 1], axis_name='patch', perm=sides)  127 us
    all_gather x1, waiting for transfers between devices, on_device(): lax.all_gather(w_query, 'patch', axis=0, tiled=True)  121 us
    all_gather x1, waiting for transfers between devices, on_device(): lax.all_gather(w_out, 'patch', axis=1, tiled=True)  103 us
    reduce_scatter x1, waiting for transfers between devices, on_device(): lax.psum_scatter(partial_out.astype(jnp.bfloat16), 'tp', scatter_dimensio...  50.8 us
    all_gather x1, waiting for transfers between devices, on_device(): lax.all_gather(w_key, 'patch', axis=0, tiled=True)  50.5 us
    all_gather x1, waiting for transfers between devices, on_device(): lax.all_gather(w_value, 'patch', axis=0, tiled=True)  46.2 us
    all_gather x1, waiting for transfers between devices, on_device(): lax.all_gather(layer_in, 'tp', axis=1, tiled=True)  22.8 us
    dot_general x1, matrix products, on_device(): picked = jnp.dot(owned_rows, unembed, preferred_element_type=jnp.float32)  17.1 us
  transfers between devices with their start and end apart: 24, of which 22 were waited for; matrix products, arithmetic and copies ran while one was open for 14% of the time, Pallas kernels for 0%

profile of v1, /device:TPU:0, one launch (start us, length us, event | category | flops | bytes accessed | tf_op | source)
XLA Modules:
  0.0 671.9 jit_solution(3826801778822679739)
XLA Ops:
  7.4 0.5 collective-permute-start
  7.9 9.3 %collective-permute-done = bf16[2,32,2048]{2,1,0:T(8,128)(2,1)S(1)} collective-permute-done((bf16[2,32,2048]{2,1,0:T(8,128)(2,1)}, bf16[2,32,2048]{2,1,0:T(8,128)(2,1)S(1)}, u32[]{:S(2)}, u32[]{:S(2)}) %collective-permute-start) | collective-permute-done | bytes 262176 | tf_op jit(solution)/shard_map/ppermute | solution.py:76
  17.2 8.5 %collective-permute-done.1 = bf16[2,32,2048]{2,1,0:T(8,128)(2,1)S(1)} collective-permute-done((bf16[2,32,2048]{2,1,0:T(8,128)(2,1)S(1)}, bf16[2,32,2048]{2,1,0:T(8,128)(2,1)S(1)}, u32[]{:S(2)}, u32[]{:S(2)}) %collective-permute-start.1) | collective-permute-done | bytes 262176 | tf_op jit(solution)/shard_map/ppermute | solution.py:76
  25.6 8.5 %collective-permute-done.2 = bf16[2,32,2048]{2,1,0:T(8,128)(2,1)S(1)} collective-permute-done((bf16[2,32,2048]{2,1,0:T(8,128)(2,1)S(1)}, bf16[2,32,2048]{2,1,0:T(8,128)(2,1)S(1)}, u32[]{:S(2)}, u32[]{:S(2)}) %collective-permute-start.2) | collective-permute-done | bytes 262176 | tf_op jit(solution)/shard_map/ppermute | solution.py:76
  34.1 8.5 %collective-permute-done.3 = bf16[2,32,2048]{2,1,0:T(8,128)(2,1)S(1)} collective-permute-done((bf16[2,32,2048]{2,1,0:T(8,128)(2,1)S(1)}, bf16[2,32,2048]{2,1,0:T(8,128)(2,1)S(1)}, u32[]{:S(2)}, u32[]{:S(2)}) %collective-permute-start.3) | collective-permute-done | bytes 262176 | tf_op jit(solution)/shard_map/ppermute | solution.py:76
  42.6 8.5 %collective-permute-done.4 = bf16[2,32,2048]{2,1,0:T(8,128)(2,1)S(1)} collective-permute-done((bf16[2,32,2048]{2,1,0:T(8,128)(2,1)S(1)}, bf16[2,32,2048]{2,1,0:T(8,128)(2,1)S(1)}, u32[]{:S(2)}, u32[]{:S(2)}) %collective-permute-start.4) | collective-permute-done | bytes 262176 | tf_op jit(solution)/shard_map/ppermute | solution.py:76
  51.1 8.5 %collective-permute-done.5 = bf16[2,32,2048]{2,1,0:T(8,128)(2,1)S(1)} collective-permute-done((bf16[2,32,2048]{2,1,0:T(8,128)(2,1)S(1)}, bf16[2,32,2048]{2,1,0:T(8,128)(2,1)S(1)}, u32[]{:S(2)}, u32[]{:S(2)}) %collective-permute-start.5) | collective-permute-done | bytes 262176 | tf_op jit(solution)/shard_map/ppermute | solution.py:76
  59.6 8.5 %collective-permute-done.6 = bf16[2,32,2048]{2,1,0:T(8,128)(2,1)S(1)} collective-permute-done((bf16[2,32,2048]{2,1,0:T(8,128)(2,1)S(1)}, bf16[2,32,2048]{2,1,0:T(8,128)(2,1)S(1)}, u32[]{:S(2)}, u32[]{:S(2)}) %collective-permute-start.6) | collective-permute-done | bytes 262176 | tf_op jit(solution)/shard_map/ppermute | solution.py:76
  68.1 8.5 %collective-permute-done.7 = bf16[2,32,2048]{2,1,0:T(8,128)(2,1)S(1)} collective-permute-done((bf16[2,32,2048]{2,1,0:T(8,128)(2,1)S(1)}, bf16[2,32,2048]{2,1,0:T(8,128)(2,1)S(1)}, u32[]{:S(2)}, u32[]{:S(2)}) %collective-permute-start.7) | collective-permute-done | bytes 262176 | tf_op jit(solution)/shard_map/ppermute | solution.py:76
  76.6 8.5 %collective-permute-done.8 = bf16[2,32,2048]{2,1,0:T(8,128)(2,1)S(1)} collective-permute-done((bf16[2,32,2048]{2,1,0:T(8,128)(2,1)S(1)}, bf16[2,32,2048]{2,1,0:T(8,128)(2,1)S(1)}, u32[]{:S(2)}, u32[]{:S(2)}) %collective-permute-start.8) | collective-permute-done | bytes 262176 | tf_op jit(solution)/shard_map/ppermute | solution.py:76
  85.1 8.5 %collective-permute-done.9 = bf16[2,32,2048]{2,1,0:T(8,128)(2,1)S(1)} collective-permute-done((bf16[2,32,2048]{2,1,0:T(8,128)(2,1)S(1)}, bf16[2,32,2048]{2,1,0:T(8,128)(2,1)S(1)}, u32[]{:S(2)}, u32[]{:S(2)}) %collective-permute-start.9) | collective-permute-done | bytes 262176 | tf_op jit(solution)/shard_map/ppermute | solution.py:76
  93.6 8.5 %collective-permute-done.10 = bf16[2,32,2048]{2,1,0:T(8,128)(2,1)S(1)} collective-permute-done((bf16[2,32,2048]{2,1,0:T(8,128)(2,1)S(1)}, bf16[2,32,2048]{2,1,0:T(8,128)(2,1)S(1)}, u32[]{:S(2)}, u32[]{:S(2)}) %collective-permute-start.10) | collective-permute-done | bytes 262176 | tf_op jit(solution)/shard_map/ppermute | solution.py:76
  102.1 8.5 %collective-permute-done.11 = bf16[2,32,2048]{2,1,0:T(8,128)(2,1)S(1)} collective-permute-done((bf16[2,32,2048]{2,1,0:T(8,128)(2,1)S(1)}, bf16[2,32,2048]{2,1,0:T(8,128)(2,1)S(1)}, u32[]{:S(2)}, u32[]{:S(2)}) %collective-permute-start.11) | collective-permute-done | bytes 262176 | tf_op jit(solution)/shard_map/ppermute | solution.py:76
  110.6 8.5 %collective-permute-done.12 = bf16[2,32,2048]{2,1,0:T(8,128)(2,1)S(1)} collective-permute-done((bf16[2,32,2048]{2,1,0:T(8,128)(2,1)S(1)}, bf16[2,32,2048]{2,1,0:T(8,128)(2,1)S(1)}, u32[]{:S(2)}, u32[]{:S(2)}) %collective-permute-start.12) | collective-permute-done | bytes 262176 | tf_op jit(solution)/shard_map/ppermute | solution.py:76
  119.1 0.7 copy-done.4
  120.4 7.9 %collective-permute-done.13 = bf16[2,32,2048]{2,1,0:T(8,128)(2,1)} collective-permute-done((bf16[2,32,2048]{2,1,0:T(8,128)(2,1)S(1)}, bf16[2,32,2048]{2,1,0:T(8,128)(2,1)}, u32[]{:S(2)}, u32[]{:S(2)}) %collective-permute-start.13) | collective-permute-done | bytes 262176 | tf_op jit(solution)/shard_map/ppermute | solution.py:76
  128.4 0.7 and_bitcast_fusion.1
  129.1 8.1 %collective-permute-done.14 = bf16[2,32,2048]{2,1,0:T(8,128)(2,1)} collective-permute-done((bf16[2,32,2048]{2,1,0:T(8,128)(2,1)}, bf16[2,32,2048]{2,1,0:T(8,128)(2,1)}, u32[]{:S(2)}, u32[]{:S(2)}) %collective-permute-start.14) | collective-permute-done | bytes 262176 | tf_op jit(solution)/shard_map/ppermute | solution.py:76
  137.2 1.0 constant_dynamic-update-slice_fusion.31
  138.2 1.0 constant_dynamic-update-slice_fusion.30
  139.1 1.0 constant_dynamic-update-slice_fusion.29
  140.4 1.0 constant_dynamic-update-slice_fusion.16
  141.4 1.0 constant_dynamic-update-slice_fusion.15
  142.4 1.0 constant_dynamic-update-slice_fusion.14
  143.8 3.2 copy-done.1
  147.0 1.9 fusion.11
  149.0 0.7 all-gather.11.cloned.1.call-update
  149.8 0.7 all-gather.9.cloned.1.call-update
  150.5 0.5 all-gather.13.cloned.1.call-update
  151.1 0.5 all-gather.15.cloned.1.call-update
  151.7 17.1 %fusion.7 = f32[32,8,32,128]{3,1,2,0:T(8,128)S(1)} fusion(bf16[4008,4096]{1,0:T(8,128)(2,1)} %param.23, s32[4008]{0:T(1024)S(1)} %iota_add_fusion, s32[256]{0:T(256)S(1)} %copy-done.9), kind=kOutput, calls=%fused_computation.18 | convolution fusion | flops 8406411264 | bytes 37044896 | tf_op jit(solution)/shard_map/dot_general | solution.py:124
  168.8 2.7 copy.44
  171.5 5.2 copy.35
  176.8 4.7 all_gather.22
  181.9 22.8 %all-gather.7.cloned.1.call-done = bf16[512,4096]{1,0:T(8,128)(2,1)} async-done(((bf16[512,2048]{1,0:T(8,128)(2,1)}), bf16[512,4096]{1,0:T(8,128)(2,1)}) %all-gather.7.cloned.1.call-update) | async-done | bytes 4194320 | tf_op jit(solution)/shard_map/all_gather | solution.py:83
  204.7 3.1 fusion.1
  207.8 50.5 %all-gather.11.cloned.1.call-done = bf16[4096,512]{1,0:T(8,128)(2,1)} async-done(((bf16[256,512]{1,0:T(8,128)(2,1)}), bf16[4096,512]{1,0:T(8,128)(2,1)}) %all-gather.11.cloned.1.call-update) | async-done | bytes 4194320 | tf_op jit(solution)/shard_map/all_gather | solution.py:96
  258.3 5.8 fusion.36
  264.1 0.4 reshape.117
  264.5 0.6 fusion.39
  265.1 46.2 %all-gather.9.cloned.1.call-done = bf16[4096,512]{1,0:T(8,128)(2,1)} async-done(((bf16[256,512]{1,0:T(8,128)(2,1)}), bf16[4096,512]{1,0:T(8,128)(2,1)}) %all-gather.9.cloned.1.call-update) | async-done | bytes 4194320 | tf_op jit(solution)/shard_map/all_gather | solution.py:101
  311.4 6.7 convolution_convert_fusion.1
  318.0 0.3 subtract_convert_fusion.1
  318.3 1.2 reshape.116
  319.5 120.5 %all-gather.13.cloned.1.call-done = bf16[4096,2048]{1,0:T(8,128)(2,1)} async-done(((bf16[256,2048]{1,0:T(8,128)(2,1)}), bf16[4096,2048]{1,0:T(8,128)(2,1)}) %all-gather.13.cloned.1.call-update) | async-done | bytes 16777232 | tf_op jit(solution)/shard_map/all_gather | solution.py:91
  440.1 13.3 %convolution_bitcast_fusion = f32[64,8,16,128]{3,1,2,0:T(8,128)S(1)} fusion(bf16[4096,2048]{1,0:T(8,128)(2,1)} %all-gather.13.cloned.1.call-done, bf16[512,4096]{1,0:T(8,128)(2,1)} %all-gather.7.cloned.1.call-done, f32[4096]{0:T(1024)S(1)} %convert_element_type.59, f32[512]{0:T(512)S(1)} %add_rsqrt_fusion.1), kind=kOutput, calls=%fused_computation.19 | convolution fusion | flops 8598323200 | bytes 25184256 | tf_op jit(solution)/shard_map/dot_general | solution.py:89
  453.4 0.9 copy.43
  454.3 1.4 subtract_convert_fusion
  455.7 0.5 copy.30
  456.3 0.5 copy.31
  456.8 1.6 fusion.12
  458.4 1.1 fusion.40
  459.5 2.1 convert_bitcast_fusion
  461.6 3.4 copy.34
  465.1 2.8 reshape.119
  467.9 103.2 %all-gather.15.cloned.1.call-done = bf16[2048,4096]{1,0:T(8,128)(2,1)} async-done(((bf16[2048,256]{1,0:T(8,128)(2,1)}), bf16[2048,4096]{1,0:T(8,128)(2,1)}) %all-gather.15.cloned.1.call-update) | async-done | bytes 16777232 | tf_op jit(solution)/shard_map/all_gather | solution.py:107
  571.1 14.4 %convolution_convert_fusion = bf16[512,4096]{1,0:T(8,128)(2,1)} fusion(bf16[512,2048]{1,0:T(8,128)(2,1)} %reshape.119, bf16[2048,4096]{1,0:T(8,128)(2,1)} %all-gather.15.cloned.1.call-done), kind=kOutput, calls=%fused_computation.6 | convolution fusion | flops 8592031744 | bytes 23068672 | tf_op jit(solution)/shard_map/dot_general | solution.py:105
  585.6 1.5 convert_element_type.69
  587.3 50.8 %reduce-scatter.4.cloned.1.call-done = bf16[512,2048]{1,0:T(8,128)(2,1)} async-done(((bf16[512,4096]{1,0:T(8,128)(2,1)}), bf16[512,2048]{1,0:T(8,128)(2,1)}) %reduce-scatter.4.cloned.1.call-update) | async-done | bytes 2097168 | tf_op jit(solution)/shard_map/reduce_scatter | solution.py:110
  638.2 3.3 multiply_reduce_fusion
  641.4 4.9 psum.7
  646.4 4.4 fusion.25
  650.9 11.8 %reduce-scatter.8.cloned.1.call-done = bf16[256,256]{1,0:T(8,128)(2,1)} async-done(((bf16[512,256]{1,0:T(8,128)(2,1)}), bf16[256,256]{1,0:T(8,128)(2,1)}) %reduce-scatter.8.cloned.1.call-update) | async-done | bytes 131088 | tf_op jit(solution)/shard_map/reduce_scatter | solution.py:140
  662.7 1.6 subtract_bitcast_fusion
  (84 shorter events, 1.4 us)
Async XLA Ops:
  7.4 136.4 %copy-start.3 = (bf16[2,32,2048]{2,1,0:T(8,128)(2,1)S(1)}, bf16[2,32,2048]{2,1,0:T(8,128)(2,1)}, u32[]{:S(2)}) copy-start(bf16[2,32,2048]{2,1,0:T(8,128)(2,1)} %param.14) | copy-start | bytes 786436
  7.4 197.3 %all-gather.7.cloned.1.call-start = ((), (), s32[]{:S(2)}) async-start(), calls=%async_computation.3 | async-start | bytes 6291456 | tf_op jit(solution)/shard_map/all_gather | solution.py:83
  7.4 9.8 %collective-permute-start = (bf16[2,32,2048]{2,1,0:T(8,128)(2,1)}, bf16[2,32,2048]{2,1,0:T(8,128)(2,1)S(1)}, u32[]{:S(2)}, u32[]{:S(2)}) collective-permute-start(bf16[2,32,2048]{2,1,0:T(8,128)(2,1)} %param.14), channel_id=1, source_target_pairs={{0,2},{2,4},{4,6},{6,8},{8,10},{10,12},{12,14},{14,16},{16,18},{18... | collective-permute-start | bytes 786440 | tf_op jit(solution)/shard_map/ppermute | solution.py:76
  17.1 8.5 %collective-permute-start.1 = (bf16[2,32,2048]{2,1,0:T(8,128)(2,1)S(1)}, bf16[2,32,2048]{2,1,0:T(8,128)(2,1)S(1)}, u32[]{:S(2)}, u32[]{:S(2)}) collective-permute-start(bf16[2,32,2048]{2,1,0:T(8,128)(2,1)S(1)} %collective-permute-done), channel_id=1, source_target_pairs={{0,2},{2,4},{4,6},{6,8},{8,10},{10,12},{12,14},{14,16},{16,18},{18... | collective-permute-start | bytes 786440 | tf_op jit(solution)/shard_map/ppermute | solution.py:76
  25.6 8.5 %collective-permute-start.2 = (bf16[2,32,2048]{2,1,0:T(8,128)(2,1)S(1)}, bf16[2,32,2048]{2,1,0:T(8,128)(2,1)S(1)}, u32[]{:S(2)}, u32[]{:S(2)}) collective-permute-start(bf16[2,32,2048]{2,1,0:T(8,128)(2,1)S(1)} %collective-permute-done.1), channel_id=1, source_target_pairs={{0,2},{2,4},{4,6},{6,8},{8,10},{10,12},{12,14},{14,16},{16,18},{18... | collective-permute-start | bytes 786440 | tf_op jit(solution)/shard_map/ppermute | solution.py:76
  34.1 8.5 %collective-permute-start.3 = (bf16[2,32,2048]{2,1,0:T(8,128)(2,1)S(1)}, bf16[2,32,2048]{2,1,0:T(8,128)(2,1)S(1)}, u32[]{:S(2)}, u32[]{:S(2)}) collective-permute-start(bf16[2,32,2048]{2,1,0:T(8,128)(2,1)S(1)} %collective-permute-done.2), channel_id=1, source_target_pairs={{0,2},{2,4},{4,6},{6,8},{8,10},{10,12},{12,14},{14,16},{16,18},{18... | collective-permute-start | bytes 786440 | tf_op jit(solution)/shard_map/ppermute | solution.py:76
  42.6 8.5 %collective-permute-start.4 = (bf16[2,32,2048]{2,1,0:T(8,128)(2,1)S(1)}, bf16[2,32,2048]{2,1,0:T(8,128)(2,1)S(1)}, u32[]{:S(2)}, u32[]{:S(2)}) collective-permute-start(bf16[2,32,2048]{2,1,0:T(8,128)(2,1)S(1)} %collective-permute-done.3), channel_id=1, source_target_pairs={{0,2},{2,4},{4,6},{6,8},{8,10},{10,12},{12,14},{14,16},{16,18},{18... | collective-permute-start | bytes 786440 | tf_op jit(solution)/shard_map/ppermute | solution.py:76
  51.1 8.5 %collective-permute-start.5 = (bf16[2,32,2048]{2,1,0:T(8,128)(2,1)S(1)}, bf16[2,32,2048]{2,1,0:T(8,128)(2,1)S(1)}, u32[]{:S(2)}, u32[]{:S(2)}) collective-permute-start(bf16[2,32,2048]{2,1,0:T(8,128)(2,1)S(1)} %collective-permute-done.4), channel_id=1, source_target_pairs={{0,2},{2,4},{4,6},{6,8},{8,10},{10,12},{12,14},{14,16},{16,18},{18... | collective-permute-start | bytes 786440 | tf_op jit(solution)/shard_map/ppermute | solution.py:76
  59.6 8.5 %collective-permute-start.6 = (bf16[2,32,2048]{2,1,0:T(8,128)(2,1)S(1)}, bf16[2,32,2048]{2,1,0:T(8,128)(2,1)S(1)}, u32[]{:S(2)}, u32[]{:S(2)}) collective-permute-start(bf16[2,32,2048]{2,1,0:T(8,128)(2,1)S(1)} %collective-permute-done.5), channel_id=1, source_target_pairs={{0,2},{2,4},{4,6},{6,8},{8,10},{10,12},{12,14},{14,16},{16,18},{18... | collective-permute-start | bytes 786440 | tf_op jit(solution)/shard_map/ppermute | solution.py:76
  68.1 8.5 %collective-permute-start.7 = (bf16[2,32,2048]{2,1,0:T(8,128)(2,1)S(1)}, bf16[2,32,2048]{2,1,0:T(8,128)(2,1)S(1)}, u32[]{:S(2)}, u32[]{:S(2)}) collective-permute-start(bf16[2,32,2048]{2,1,0:T(8,128)(2,1)S(1)} %collective-permute-done.6), channel_id=1, source_target_pairs={{0,2},{2,4},{4,6},{6,8},{8,10},{10,12},{12,14},{14,16},{16,18},{18... | collective-permute-start | bytes 786440 | tf_op jit(solution)/shard_map/ppermute | solution.py:76
  76.6 8.5 %collective-permute-start.8 = (bf16[2,32,2048]{2,1,0:T(8,128)(2,1)S(1)}, bf16[2,32,2048]{2,1,0:T(8,128)(2,1)S(1)}, u32[]{:S(2)}, u32[]{:S(2)}) collective-permute-start(bf16[2,32,2048]{2,1,0:T(8,128)(2,1)S(1)} %collective-permute-done.7), channel_id=1, source_target_pairs={{0,2},{2,4},{4,6},{6,8},{8,10},{10,12},{12,14},{14,16},{16,18},{18... | collective-permute-start | bytes 786440 | tf_op jit(solution)/shard_map/ppermute | solution.py:76
  85.1 8.5 %collective-permute-start.9 = (bf16[2,32,2048]{2,1,0:T(8,128)(2,1)S(1)}, bf16[2,32,2048]{2,1,0:T(8,128)(2,1)S(1)}, u32[]{:S(2)}, u32[]{:S(2)}) collective-permute-start(bf16[2,32,2048]{2,1,0:T(8,128)(2,1)S(1)} %collective-permute-done.8), channel_id=1, source_target_pairs={{0,2},{2,4},{4,6},{6,8},{8,10},{10,12},{12,14},{14,16},{16,18},{18... | collective-permute-start | bytes 786440 | tf_op jit(solution)/shard_map/ppermute | solution.py:76
  93.6 8.5 %collective-permute-start.10 = (bf16[2,32,2048]{2,1,0:T(8,128)(2,1)S(1)}, bf16[2,32,2048]{2,1,0:T(8,128)(2,1)S(1)}, u32[]{:S(2)}, u32[]{:S(2)}) collective-permute-start(bf16[2,32,2048]{2,1,0:T(8,128)(2,1)S(1)} %collective-permute-done.9), channel_id=1, source_target_pairs={{0,2},{2,4},{4,6},{6,8},{8,10},{10,12},{12,14},{14,16},{16,18},{18... | collective-permute-start | bytes 786440 | tf_op jit(solution)/shard_map/ppermute | solution.py:76
  102.1 8.5 %collective-permute-start.11 = (bf16[2,32,2048]{2,1,0:T(8,128)(2,1)S(1)}, bf16[2,32,2048]{2,1,0:T(8,128)(2,1)S(1)}, u32[]{:S(2)}, u32[]{:S(2)}) collective-permute-start(bf16[2,32,2048]{2,1,0:T(8,128)(2,1)S(1)} %collective-permute-done.10), channel_id=1, source_target_pairs={{0,2},{2,4},{4,6},{6,8},{8,10},{10,12},{12,14},{14,16},{16,18},{18... | collective-permute-start | bytes 786440 | tf_op jit(solution)/shard_map/ppermute | solution.py:76
  110.6 8.5 %collective-permute-start.12 = (bf16[2,32,2048]{2,1,0:T(8,128)(2,1)S(1)}, bf16[2,32,2048]{2,1,0:T(8,128)(2,1)S(1)}, u32[]{:S(2)}, u32[]{:S(2)}) collective-permute-start(bf16[2,32,2048]{2,1,0:T(8,128)(2,1)S(1)} %collective-permute-done.11), channel_id=1, source_target_pairs={{0,2},{2,4},{4,6},{6,8},{8,10},{10,12},{12,14},{14,16},{16,18},{18... | collective-permute-start | bytes 786440 | tf_op jit(solution)/shard_map/ppermute | solution.py:76
  119.1 0.7 copy-start.4
  119.8 8.6 %collective-permute-start.13 = (bf16[2,32,2048]{2,1,0:T(8,128)(2,1)S(1)}, bf16[2,32,2048]{2,1,0:T(8,128)(2,1)}, u32[]{:S(2)}, u32[]{:S(2)}) collective-permute-start(bf16[2,32,2048]{2,1,0:T(8,128)(2,1)S(1)} %collective-permute-done.12), channel_id=1, source_target_pairs={{0,2},{2,4},{4,6},{6,8},{8,10},{10,12},{12,14},{14,16},{16,18},{18... | collective-permute-start | bytes 786440 | tf_op jit(solution)/shard_map/ppermute | solution.py:76
  128.4 8.8 %collective-permute-start.14 = (bf16[2,32,2048]{2,1,0:T(8,128)(2,1)}, bf16[2,32,2048]{2,1,0:T(8,128)(2,1)}, u32[]{:S(2)}, u32[]{:S(2)}) collective-permute-start(bf16[2,32,2048]{2,1,0:T(8,128)(2,1)} %collective-permute-done.13), channel_id=1, source_target_pairs={{0,2},{2,4},{4,6},{6,8},{8,10},{10,12},{12,14},{14,16},{16,18},{18... | collective-permute-start | bytes 786440 | tf_op jit(solution)/shard_map/ppermute | solution.py:76
  129.1 14.3 %copy-start.5 = (bf16[2,32,2048]{2,1,0:T(8,128)(2,1)S(1)}, bf16[2,32,2048]{2,1,0:T(8,128)(2,1)}, u32[]{:S(2)}) copy-start(bf16[2,32,2048]{2,1,0:T(8,128)(2,1)} %copy-done.4) | copy-start | bytes 786436
  129.1 18.0 %copy-start.2 = (bf16[512,2048]{1,0:T(8,128)(2,1)S(1)}, bf16[512,2048]{1,0:T(8,128)(2,1)}, u32[]{:S(2)}) copy-start(bf16[512,2048]{1,0:T(8,128)(2,1)} %param.13) | copy-start | bytes 6291460
  143.5 8.2 %copy-start.9 = (s32[256]{0:T(256)S(1)}, s32[256]{0:T(256)}, u32[]{:S(2)}) copy-start(s32[256]{0:T(256)} %param.24) | copy-start | bytes 3076
  143.8 3.2 copy-start.1
  149.0 109.3 %all-gather.11.cloned.1.call-start = ((), (), s32[]{:S(2)}) async-start(), calls=%async_computation.5 | async-start | bytes 4456448 | tf_op jit(solution)/shard_map/all_gather | solution.py:96
  149.7 161.6 %all-gather.9.cloned.1.call-start = ((), (), s32[]{:S(2)}) async-start(), calls=%async_computation.4 | async-start | bytes 4456448 | tf_op jit(solution)/shard_map/all_gather | solution.py:101
  150.5 289.6 %all-gather.13.cloned.1.call-start = ((), (), s32[]{:S(2)}) async-start(), calls=%async_computation.6 | async-start | bytes 17825792 | tf_op jit(solution)/shard_map/all_gather | solution.py:91
  151.0 420.1 %all-gather.15.cloned.1.call-start = ((), (), s32[]{:S(2)}) async-start(), calls=%async_computation.7 | async-start | bytes 17825792 | tf_op jit(solution)/shard_map/all_gather | solution.py:107
  151.6 434.0 %reduce-scatter.6.cloned.1.call-start = ((), (), s32[]{:S(2)}) async-start(), calls=%async_computation.9 | async-start | bytes 4325376 | tf_op jit(solution)/shard_map/reduce_scatter | solution.py:133
  171.5 5.4 copy-start.7
  176.7 461.4 %reduce-scatter.4.cloned.1.call-start = ((), (), s32[]{:S(2)}) async-start(), calls=%async_computation.8 | async-start | bytes 6291456 | tf_op jit(solution)/shard_map/reduce_scatter | solution.py:110
  467.9 119.4 %copy-start.8 = (bf16[2048]{0:T(1024)(128)(2,1)S(1)}, bf16[2048]{0:T(1024)(128)(2,1)}, u32[]{:S(2)}) copy-start(bf16[2048]{0:T(1024)(128)(2,1)} %param.18) | copy-start | bytes 12292
  467.9 170.3 %copy-start = (bf16[512,2048]{1,0:T(8,128)(2,1)S(1)}, bf16[512,2048]{1,0:T(8,128)(2,1)}, u32[]{:S(2)}) copy-start(bf16[512,2048]{1,0:T(8,128)(2,1)} %fusion.11) | copy-start | bytes 6291460
  585.6 60.8 %all-gather.17.cloned.1.call-start = ((), (), s32[]{:S(2)}) async-start(), calls=%async_computation.10 | async-start | bytes 1114112 | tf_op jit(solution)/shard_map/all_gather | solution.py:136
  587.2 75.5 %reduce-scatter.8.cloned.1.call-start = ((), (), s32[]{:S(2)}) async-start(), calls=%async_computation.11 | async-start | bytes 393216 | tf_op jit(solution)/shard_map/reduce_scatter | solution.py:140
  587.3 75.4 %copy-start.6 = (f32[256,256]{1,0:T(8,128)S(1)}, f32[256,256]{1,0:T(8,128)}, u32[]{:S(2)}) copy-start(f32[256,256]{1,0:T(8,128)} %param.25) | copy-start | bytes 786436
Sparse Core Ops, SparseCore 0:
  149.1 55.5 all-gather.6
  206.8 51.4 all-gather.10
  260.5 50.8 all-gather.8
  313.4 126.6 all-gather.12
  442.1 129.0 all-gather.14
  588.2 36.0 all-gather.16
Sparse Core Ops, SparseCore 1:
  176.8 264.5 reduce-scatter.5
  585.6 52.5 reduce-scatter.3
  650.9 11.7 reduce-scatter.7
